TPU v7x, 32 devices: a whole 2x2x4 slice. The times are simulated.
32 devices in a mesh: wave: 4 (over y, x), freq: 8 (over z, core).
Axes of the slice: x: 2, y: 2, z: 4, core: 2. Of those that a mesh axis runs over, the one named last changes fastest.
Arguments:
- waveforms: float32 [1024, 16384], P('wave', 'freq'), may hold values from -6 to 6
- pivots: int32 [2, 128], replicated, may hold values from 0 to 1023, as said below
- nodes: int32 [1024], replicated, may hold values from 0 to 16383, as said below
Outputs:
- residual: float32 [1024, 16384], P('wave', 'freq')
- basis_rows: float32 [256, 16384], P(None, 'freq')
- fitted: float32 [1024, 16384], P('wave', 'freq')
Inputs may be any that keep to these rules, and one draw needn't show every extreme that they name: `pivots`: all 256 pivot indices are different. `nodes`: all node indices are different.
All inputs are finite; a program needn't handle non-finite values.
Results may differ from a plain program's by a relative error of at most 0.0001.
Values sent between devices are 32-bit elements; how exact they have to be, the bound alone decides.
A program may use at most 64 MiB of HBM per device.

v0:
```python
import jax
import jax.numpy as jnp
from jax import lax
from jax.sharding import PartitionSpec as P

HIGH = lax.Precision.HIGH


def body(waveforms, pivots, nodes):
    rows_here, cols_here = waveforms.shape
    row_start = lax.axis_index("wave") * rows_here
    col_start = lax.axis_index("freq") * cols_here
    picks = pivots.reshape(-1)
    count = picks.shape[0]
    local_rows = picks - row_start
    inside = ((local_rows >= 0) & (local_rows < rows_here)).astype(jnp.float32)
    picked = jnp.take(waveforms, jnp.clip(local_rows, 0, rows_here - 1), axis=0) * inside[:, None]
    pivot_rows = lax.psum(picked, "wave")
    columns = col_start + jnp.arange(cols_here, dtype=jnp.int32)
    node_count = jnp.sum((nodes[:, None] == columns[None, :]).astype(jnp.float32), axis=0)
    weighted = pivot_rows * node_count[None, :]
    left = jnp.concatenate([pivot_rows, waveforms], axis=0)
    right = jnp.concatenate([pivot_rows, weighted], axis=0)
    total = lax.psum(jnp.dot(left, right.T, precision=HIGH), "freq")
    gram, node_gram = (total[:count, :count], total[:count, count:])
    cross, node_cross = (total[count:, :count], total[count:, count:])
    factors = jnp.linalg.cholesky(jnp.stack([gram, node_gram]))
    eye = jnp.broadcast_to(jnp.eye(count, dtype=jnp.float32), factors.shape)
    inverses = jax.scipy.linalg.solve_triangular(factors, eye, lower=True)
    hi = lax.Precision.HIGHEST
    basis_rows = jnp.dot(inverses[0], pivot_rows, precision=HIGH)
    coeffs = jnp.dot(cross, inverses[0].T, precision=hi)
    residual = waveforms - jnp.dot(coeffs, basis_rows, precision=HIGH)
    coefficients = jnp.dot(
        jnp.dot(node_cross, inverses[1].T, precision=hi), inverses[1], precision=hi
    )
    fitted = jnp.dot(coefficients, pivot_rows, precision=HIGH)
    return (residual, basis_rows, fitted)


def solution(mesh):
    in_specs = (P("wave", "freq"), P(), P())
    out_specs = (P("wave", "freq"), P(None, "freq"), P("wave", "freq"))
    return jax.shard_map(body, mesh=mesh, in_specs=in_specs, out_specs=out_specs, check_vma=False)
```

profile of v0, /device:TPU:0, one launch (start us, length us, event | category | flops | bytes accessed | tf_op | source)
XLA Modules:
  0.0 288.0 jit_solution(7392579073697744297)
XLA Ops:
  7.2 0.7 fusion.25
  7.9 0.7 compare_and_fusion
  8.6 4.0 %gather_fusion = f32[256,2048]{1,0:T(8,128)S(1)} fusion(f32[256,2048]{1,0:T(8,128)} %param.3, s32[1024]{0:T(1024)S(1)} %pad_clamp_fusion), kind=kCustom, calls=%fused_computation | custom fusion | bytes 4195328 | tf_op jit(solution)/shard_map/jit(_take)/gather | solution.py:17
  12.6 1.6 select_multiply_fusion
  14.3 0.5 copy-done.6
  14.9 0.9 convert_reduce_fusion
  15.8 70.8 %all-reduce.4.cloned.1.call-done = f32[256,2048]{1,0:T(8,128)} async-done(((f32[256,2048]{1,0:T(8,128)}), f32[256,2048]{1,0:T(8,128)}) %all-reduce.4.cloned.1.call-update) | async-done | bytes 2097168 | tf_op jit(solution)/shard_map/psum | solution.py:18
  86.6 2.0 broadcast_multiply_fusion
  88.8 4.6 %fusion = f32[512,512]{0,1:T(8,128)} fusion(f32[256,2048]{1,0:T(8,128)S(1)} %copy-done.1, f32[256,2048]{1,0:T(8,128)S(1)} %copy-done, f32[256,2048]{1,0:T(8,128)S(1)} %broadcast_multiply_fusion), kind=kOutput, calls=%fused_computation.6 | convolution fusion | flops 3223322624 | bytes 7340032 | tf_op jit(solution)/shard_map/dot_general | solution.py:24
  93.5 59.4 %all-reduce.6.cloned.1.call-done = f32[512,512]{0,1:T(8,128)} async-done(((f32[512,512]{0,1:T(8,128)}), f32[512,512]{0,1:T(8,128)}) %all-reduce.6.cloned.1.call-update) | async-done | bytes 1048592 | tf_op jit(solution)/shard_map/psum | solution.py:24
  152.9 1.1 slice_bitcast_fusion.1
  153.9 0.8 pad_maximum_fusion.4
  154.8 1.2 copy.14
  156.1 0.8 copy-done.4
  156.9 23.6 %custom-call.17 = f32[2,128,128]{2,1,0:T(8,128)S(1)} custom-call(f32[2,128,128]{2,1,0:T(8,128)S(1)} %cholesky.122), custom_call_target="Cholesky" | custom-call | tf_op jit(solution)/shard_map/jit(cholesky)/cholesky | solution.py:27
  180.6 19.7 %custom-call.18 = f32[2,1,128,128]{2,3,1,0:T(8,128)S(1)} custom-call(f32[2,1,128,128]{3,2,1,0:T(8,128)S(1)} %select_bitcast_fusion), custom_call_target="InvertDiagBlocksLowerTriangular" | custom-call | tf_op jit(solution)/shard_map/jit(cholesky)/cholesky | solution.py:27
  200.3 1.2 constant_dynamic-update-slice_fusion.1
  201.5 1.3 convolution_subtract_fusion.2
  202.8 23.5 %custom-call.19 = f32[2,128,128]{2,1,0:T(8,128)S(1)} custom-call(f32[2,128,128]{2,1,0:T(8,128)S(1)} %convolution_subtract_fusion.2), custom_call_target="Cholesky" | custom-call | tf_op jit(solution)/shard_map/jit(cholesky)/cholesky | solution.py:27
  226.7 5.3 %while.1 = (s32[]{:T(128)}, f32[2,256,256]{2,1,0:T(8,128)S(1)}, s32[2,2]{1,0:T(2,128)S(1)}, f32[2,2,128,128]{3,2,0,1:T(8,128)}, s32[]{:T(128)}) while((s32[]{:T(128)}, f32[2,256,256]{2,1,0:T(8,128)S(1)}, s32[2,2]{1,0:T(2,128)S(1)}, f32[2,2,128,128]{3,2,0,1:T(8,128)}, s32[]{:T(128)}) %tuple.30), condition=%wide.while_cond, body=%wide.while_body.sunk | while | flops 2 | bytes 263277 | solution.py:29
  226.7 0.6 fusion.45
  227.3 2.0 bitcast_dynamic-update-slice_fusion.2
  229.3 0.6 fusion.45
  229.9 2.0 bitcast_dynamic-update-slice_fusion.2
  231.9 40.1 %custom-call.20 = f32[2,2,128,128]{2,3,1,0:T(8,128)S(1)} custom-call(f32[2,2,128,128]{3,2,1,0:T(8,128)} %bitcast.62), custom_call_target="InvertDiagBlocksLowerTriangular" | custom-call | tf_op jit(solution)/shard_map/jit(_solve_triangular)/vmap()/triangular_solve | solution.py:29
  272.1 0.4 fusion.14
  272.9 0.4 fusion.13
  273.3 0.6 fusion.7
  274.3 0.6 fusion.9
  274.9 1.2 fusion.22
  276.1 2.5 convolution_subtract_fusion
  278.7 2.5 fusion.33
  (39 shorter events, 1.8 us)
Async XLA Ops:
  7.2 79.4 %all-reduce.4.cloned.1.call-start = ((), (), s32[]{:S(2)}) async-start(), calls=%async_computation | async-start | bytes 4194304 | tf_op jit(solution)/shard_map/psum | solution.py:18
  14.2 0.7 copy-start.6
  14.2 138.6 %all-reduce.6.cloned.1.call-start = ((), (), s32[]{:S(2)}) async-start(), calls=%async_computation.1 | async-start | bytes 2097152 | tf_op jit(solution)/shard_map/psum | solution.py:24
  15.8 72.8 %copy-start = (f32[256,2048]{1,0:T(8,128)S(1)}, f32[256,2048]{1,0:T(8,128)}, u32[]{:S(2)}) copy-start(f32[256,2048]{1,0:T(8,128)} %param.3) | copy-start | bytes 6291460
  86.6 2.2 copy-start.1
  156.1 0.8 copy-start.4
  272.1 1.3 copy-start.5
  272.9 2.0 copy-start.2
  276.1 2.5 copy-start.3
Sparse Core Ops, SparseCore 0:
  14.3 72.1 all-reduce.3
  93.5 59.2 all-reduce.5
where the time goes:
time: 288 us
  waiting for transfers between devices  130 us (45%)
  other arithmetic  114 us (40%)
  matrix products  16.1 us (6%)
  between operations  14.3 us (5%)
  local copies, waits for them, and re-layouts  13.3 us (5%)
    psum x1, waiting for transfers between devices, body(): pivot_rows = lax.psum(picked, 'wave')  70.8 us
    another operation x10, other arithmetic, body(): factors = jnp.linalg.cholesky(jnp.stack([gram, node_gram]))  67.8 us
    psum x1, waiting for transfers between devices, body(): total = lax.psum(jnp.dot(left, right.T, precision=HIGH), 'freq')  59.4 us
    another operation x4, other arithmetic, body(): inverses = jax.scipy.linalg.solve_triangular(factors, eye, lower=True)  40.3 us
  transfers between devices with their start and end apart: 2, of which 2 were waited for; matrix products, arithmetic and copies ran while one was open for 0% of the time, Pallas kernels for 0%

commit v1 on v0

--- a/solution.py
+++ b/solution.py
@@ -4,6 +4,15 @@
 from jax.sharding import PartitionSpec as P
 
 HIGH = lax.Precision.HIGH
+
+
+def add_in_pairs(x, axis):
+    n_dev = lax.axis_size(axis)
+    summed, stride = (x, 1)
+    while stride < n_dev:
+        summed = summed + lax.ppermute(summed, axis, [(i, i ^ stride) for i in range(n_dev)])
+        stride = 2 * stride
+    return summed
 
 
 def body(waveforms, pivots, nodes):
@@ -15,7 +24,7 @@
     local_rows = picks - row_start
     inside = ((local_rows >= 0) & (local_rows < rows_here)).astype(jnp.float32)
     picked = jnp.take(waveforms, jnp.clip(local_rows, 0, rows_here - 1), axis=0) * inside[:, None]
-    pivot_rows = lax.psum(picked, "wave")
+    pivot_rows = add_in_pairs(picked, "wave")
     columns = col_start + jnp.arange(cols_here, dtype=jnp.int32)
     node_count = jnp.sum((nodes[:, None] == columns[None, :]).astype(jnp.float32), axis=0)
     weighted = pivot_rows * node_count[None, :]

time: 288 us -> 317 us (1.10)
  waiting for transfers between devices: 130 us -> 151 us
  starting transfers between devices: 0.08 us -> 4.84 us
    ppermute x0 -> x2, waiting for transfers between devices: none -> 90 us  [add_in_pairs(): lax.ppermute(summed, axis, [(i, i ^ stride) for i in range(n_dev)])]
    psum x1 -> x0, waiting for transfers between devices: 70.8 us -> none  [body(): pivot_rows = lax.psum(picked, 'wave')]
    ppermute x0 -> x2, starting transfers between devices: none -> 4.8 us  [add_in_pairs(): lax.ppermute(summed, axis, [(i, i ^ stride) for i in range(n_dev)])]
  transfers between devices with their start and end apart: 2 -> 3, of which waited for: 2 -> 3; matrix products, arithmetic and copies ran while one was open for 0% -> 0% of each run, Pallas kernels for 0% -> 0%
where the time goes in v1:
time: 317 us; the launch traced here: 316 us
  waiting for transfers between devices  151 us (48%)
  other arithmetic  115 us (36%)
  matrix products  17.7 us (6%)
  between operations  14.3 us (5%)
  local copies, waits for them, and re-layouts  13.7 us (4%)
  starting transfers between devices  4.84 us (2%)
    ppermute x2, waiting for transfers between devices, add_in_pairs(): lax.ppermute(summed, axis, [(i, i ^ stride) for i in range(n_dev)])  90 us
    another operation x10, other arithmetic, body(): factors = jnp.linalg.cholesky(jnp.stack([gram, node_gram]))  67.8 us
    psum x1, waiting for transfers between devices, body(): total = lax.psum(jnp.dot(left, right.T, precision=HIGH), 'freq')  60.6 us
    another operation x4, other arithmetic, body(): inverses = jax.scipy.linalg.solve_triangular(factors, eye, lower=True)  40.3 us
  transfers between devices with their start and end apart: 3, of which 3 were waited for; matrix products, arithmetic and copies ran while one was open for 0% of the time, Pallas kernels for 0%

profile of v1, /device:TPU:0, one launch (start us, length us, event | category | flops | bytes accessed | tf_op | source)
XLA Modules:
  0.0 316.3 jit_solution(12016853093428532498)
XLA Ops:
  7.2 0.7 fusion.25
  7.9 0.7 compare_and_fusion
  8.6 4.0 %gather_fusion = f32[256,2048]{1,0:T(8,128)S(1)} fusion(f32[256,2048]{1,0:T(8,128)} %param.3, s32[1024]{0:T(1024)S(1)} %pad_clamp_fusion), kind=kCustom, calls=%fused_computation | custom fusion | bytes 4195328 | tf_op jit(solution)/shard_map/jit(_take)/gather | solution.py:26
  12.9 3.0 collective-permute-start
  15.9 45.6 %collective-permute-done = f32[256,2048]{1,0:T(8,128)S(1)} collective-permute-done((f32[256,2048]{1,0:T(8,128)S(1)}, f32[256,2048]{1,0:T(8,128)S(1)}, u32[]{:S(2)}, u32[]{:S(2)}) %collective-permute-start) | collective-permute-done | bytes 2097184 | tf_op jit(solution)/shard_map/ppermute | solution.py:13
  61.6 1.7 fusion.44
  63.3 1.8 collective-permute-start.1
  65.1 0.9 convert_reduce_fusion
  66.0 44.4 %collective-permute-done.1 = f32[256,2048]{1,0:T(8,128)} collective-permute-done((f32[256,2048]{1,0:T(8,128)}, f32[256,2048]{1,0:T(8,128)}, u32[]{:S(2)}, u32[]{:S(2)}) %collective-permute-start.1) | collective-permute-done | bytes 2097184 | tf_op jit(solution)/shard_map/ppermute | solution.py:13
  110.4 2.7 broadcast_multiply_fusion
  113.1 1.3 copy-done.1
  114.4 4.6 %fusion = f32[512,512]{0,1:T(8,128)} fusion(f32[256,2048]{1,0:T(8,128)S(1)} %get-tuple-element.22, f32[256,2048]{1,0:T(8,128)S(1)} %copy-done, f32[256,2048]{1,0:T(8,128)S(1)} %get-tuple-element.21), kind=kOutput, calls=%fused_computation.6 | convolution fusion | flops 3223322624 | bytes 7340032 | tf_op jit(solution)/shard_map/dot_general | solution.py:33
  119.1 60.6 %all-reduce.3.cloned.1.call-done = f32[512,512]{0,1:T(8,128)} async-done(((f32[512,512]{0,1:T(8,128)}), f32[512,512]{0,1:T(8,128)}) %all-reduce.3.cloned.1.call-update) | async-done | bytes 1048592 | tf_op jit(solution)/shard_map/psum | solution.py:33
  179.7 1.1 slice_bitcast_fusion.1
  180.7 0.8 pad_maximum_fusion.4
  181.6 1.2 copy.14
  182.9 0.8 copy-done.4
  183.7 23.6 %custom-call.17 = f32[2,128,128]{2,1,0:T(8,128)S(1)} custom-call(f32[2,128,128]{2,1,0:T(8,128)S(1)} %cholesky.122), custom_call_target="Cholesky" | custom-call | tf_op jit(solution)/shard_map/jit(cholesky)/cholesky | solution.py:36
  207.4 19.7 %custom-call.18 = f32[2,1,128,128]{2,3,1,0:T(8,128)S(1)} custom-call(f32[2,1,128,128]{3,2,1,0:T(8,128)S(1)} %select_bitcast_fusion), custom_call_target="InvertDiagBlocksLowerTriangular" | custom-call | tf_op jit(solution)/shard_map/jit(cholesky)/cholesky | solution.py:36
  227.1 1.2 constant_dynamic-update-slice_fusion.1
  228.3 1.3 convolution_subtract_fusion.2
  229.6 23.5 %custom-call.19 = f32[2,128,128]{2,1,0:T(8,128)S(1)} custom-call(f32[2,128,128]{2,1,0:T(8,128)S(1)} %convolution_subtract_fusion.2), custom_call_target="Cholesky" | custom-call | tf_op jit(solution)/shard_map/jit(cholesky)/cholesky | solution.py:36
  253.5 5.2 %while.1 = (s32[]{:T(128)}, f32[2,256,256]{2,1,0:T(8,128)S(1)}, s32[2,2]{1,0:T(2,128)S(1)}, f32[2,2,128,128]{3,2,0,1:T(8,128)}, s32[]{:T(128)}) while((s32[]{:T(128)}, f32[2,256,256]{2,1,0:T(8,128)S(1)}, s32[2,2]{1,0:T(2,128)S(1)}, f32[2,2,128,128]{3,2,0,1:T(8,128)}, s32[]{:T(128)}) %tuple.31), condition=%wide.while_cond, body=%wide.while_body.sunk | while | flops 2 | bytes 263277 | solution.py:38
  253.5 0.6 fusion.46
  254.1 2.0 bitcast_dynamic-update-slice_fusion.2
  256.6 2.0 bitcast_dynamic-update-slice_fusion.2
  258.6 40.1 %custom-call.20 = f32[2,2,128,128]{2,3,1,0:T(8,128)S(1)} custom-call(f32[2,2,128,128]{3,2,1,0:T(8,128)} %bitcast.62), custom_call_target="InvertDiagBlocksLowerTriangular" | custom-call | tf_op jit(solution)/shard_map/jit(_solve_triangular)/vmap()/triangular_solve | solution.py:38
  300.0 2.8 fusion.22
  302.8 0.6 fusion.7
  303.8 2.5 fusion.33
  306.3 0.6 fusion.9
  307.0 2.5 convolution_subtract_fusion
  (41 shorter events, 3.2 us)
Async XLA Ops:
  7.2 172.5 %all-reduce.3.cloned.1.call-start = ((), (), s32[]{:S(2)}) async-start(), calls=%async_computation | async-start | bytes 2097152 | tf_op jit(solution)/shard_map/psum | solution.py:33
  12.9 52.2 %copy-start.6 = (s32[1024]{0:T(1024)S(1)}, s32[1024]{0:T(1024)}, u32[]{:S(2)}) copy-start(s32[1024]{0:T(1024)} %param.5) | copy-start | bytes 12292
  12.9 48.7 %collective-permute-start = (f32[256,2048]{1,0:T(8,128)S(1)}, f32[256,2048]{1,0:T(8,128)S(1)}, u32[]{:S(2)}, u32[]{:S(2)}) collective-permute-start(f32[256,2048]{1,0:T(8,128)S(1)} %select_multiply_fusion), channel_id=1, source_target_pairs={{0,8},{8,0},{16,24},{24,16},{1,9},{9,1},{17,25},{25,17},{2,10},{10... | collective-permute-start | bytes 6291464 | tf_op jit(solution)/shard_map/ppermute | solution.py:13
  63.3 47.1 %collective-permute-start.1 = (f32[256,2048]{1,0:T(8,128)}, f32[256,2048]{1,0:T(8,128)}, u32[]{:S(2)}, u32[]{:S(2)}) collective-permute-start(f32[256,2048]{1,0:T(8,128)} %fusion.44), channel_id=1, source_target_pairs={{0,16},{8,24},{16,0},{24,8},{1,17},{9,25},{17,1},{25,9},{2,18},{10... | collective-permute-start | bytes 6291464 | tf_op jit(solution)/shard_map/ppermute | solution.py:13
  66.0 48.4 %copy-start = (f32[256,2048]{1,0:T(8,128)S(1)}, f32[256,2048]{1,0:T(8,128)}, u32[]{:S(2)}) copy-start(f32[256,2048]{1,0:T(8,128)} %param.3) | copy-start | bytes 6291460
  113.1 1.3 copy-start.1
  182.9 0.8 copy-start.4
  300.0 2.8 copy-start.5
  300.0 3.8 %copy-start.2 = (f32[256,2048]{1,0:T(8,128)S(1)}, f32[256,2048]{1,0:T(8,128)}, u32[]{:S(2)}) copy-start(f32[256,2048]{1,0:T(8,128)} %copy-done.1) | copy-start | bytes 6291460
  302.8 4.1 %copy-start.3 = (f32[256,2048]{1,0:T(8,128)}, f32[256,2048]{1,0:T(8,128)S(1)}, u32[]{:S(2)}) copy-start(f32[256,2048]{1,0:T(8,128)S(1)} %fusion.22) | copy-start | bytes 6291460
Sparse Core Ops, SparseCore 0:
  119.1 60.5 all-reduce.2
